TPU v7x, 128 devices: a whole 4x4x4 slice. The times are simulated.
128 devices in a mesh: gx: 2 (over core), gy: 64 (over z, y, x).
Axes of the slice: x: 4, y: 4, z: 4, core: 2. Of those that a mesh axis runs over, the one named last changes fastest.
Arguments:
- right_side: float32 [128, 16384], P('gx', 'gy'), may hold values from -34 to 34, as said below
- initial: float32 [128, 16384], P('gx', 'gy'), may hold values from -0.6 to 0.6
- reaction: float32 [128, 16384], P('gx', 'gy'), may hold values from 0.05 to 0.5
- velocity_x: float32 [128, 16384], P('gx', 'gy'), may hold values from -1 to 1
- velocity_y: float32 [128, 16384], P('gx', 'gy'), may hold values from -1 to 1
Outputs:
- solution: float32 [128, 16384], P('gx', 'gy')
- residual: float32 [128, 16384], P('gx', 'gy')
Inputs may be any that keep to these rules, and one draw needn't show every extreme that they name: right_side is noise bounded by 4 in size times an envelope 0.5 + 8 g, where g is a periodic Gaussian bump of one device block's width along each dimension centred at a drawn position, so its entries lie within -34 and 34.
All inputs are finite; a program needn't handle non-finite values.
Results may differ from a plain program's by a relative error of at most 0.0075.
Values sent between devices are 32-bit elements.
A program may use at most 64 MiB of HBM per device.

v0:
```python
import jax
import jax.numpy as jnp
from jax import lax
from jax.sharding import Mesh
from jax.sharding import PartitionSpec as P

RESTART = 15
GX_GY = ("gx", "gy_0", "gy_1", "gy_2")
GY = ("gy_0", "gy_1", "gy_2")


def padded_2(cells, sides, width, closed):
    for axis, dim in sides:
        count = lax.axis_size(axis)
        ends = count if closed else count - 1
        head = lax.slice_in_dim(cells, 0, width, axis=dim)
        tail = lax.slice_in_dim(cells, cells.shape[dim] - width, cells.shape[dim], axis=dim)
        cells = jnp.concatenate(
            [
                lax.ppermute(tail, axis, [(i, (i + 1) % count) for i in range(ends)]),
                cells,
                lax.ppermute(head, axis, [((i + 1) % count, i) for i in range(ends)]),
            ],
            axis=dim,
        )
    return cells


def one_axis_at_a_time(x, axes):
    for axis in axes:
        x = lax.psum(x, axis)
    return x


def shifted(padded, offset, dimension, extent):
    row_start = 2 + offset if dimension == 0 else 2
    column_start = 2 + offset if dimension == 1 else 2
    return lax.slice(
        padded, (row_start, column_start), (row_start + extent[0], column_start + extent[1])
    )


def first_diff(padded, dimension, extent):
    outer = shifted(padded, -2, dimension, extent) - shifted(padded, 2, dimension, extent)
    inner = shifted(padded, 1, dimension, extent) - shifted(padded, -1, dimension, extent)
    return (outer + 8.0 * inner) / 12.0


def second_diff(padded, dimension, extent):
    inner = shifted(padded, 1, dimension, extent) + shifted(padded, -1, dimension, extent)
    outer = shifted(padded, 2, dimension, extent) + shifted(padded, -2, dimension, extent)
    return (16.0 * inner - outer - 30.0 * shifted(padded, 0, dimension, extent)) / 12.0


def apply_operator(field, padded_field, padded_speeds, reaction, velocity_x, velocity_y):
    extent = field.shape
    diffusion = second_diff(padded_field, 0, extent) + second_diff(padded_field, 1, extent)
    advect_x = 0.5 * (
        velocity_x * first_diff(padded_field, 0, extent)
        + first_diff(padded_speeds[0] * padded_field, 0, extent)
    )
    advect_y = 0.5 * (
        velocity_y * first_diff(padded_field, 1, extent)
        + first_diff(padded_speeds[1] * padded_field, 1, extent)
    )
    return reaction * field - diffusion + advect_x + advect_y


def least_squares(hessenberg, beta):
    columns_total = hessenberg.shape[1]
    target = jnp.where(jnp.arange(columns_total + 1) == 0, beta, 0.0)

    def rotate(column, carried):
        upper, target = carried
        top_row = upper[column]
        next_row = upper[column + 1]
        diagonal_entry = top_row[column]
        below_entry = next_row[column]
        radius = jnp.sqrt(diagonal_entry * diagonal_entry + below_entry * below_entry)
        cosine = diagonal_entry / radius
        sine_value = below_entry / radius
        upper = upper.at[column].set(cosine * top_row + sine_value * next_row)
        upper = upper.at[column + 1].set(cosine * next_row - sine_value * top_row)
        upper_value = target[column]
        lower_value = target[column + 1]
        target = target.at[column].set(cosine * upper_value + sine_value * lower_value)
        target = target.at[column + 1].set(cosine * lower_value - sine_value * upper_value)
        return (upper, target)

    upper, target = lax.fori_loop(0, columns_total, rotate, (hessenberg, target))

    def substitute(count, weights):
        row_index = columns_total - 1 - count
        known = jnp.sum(upper[row_index] * weights)
        return weights.at[row_index].set((target[row_index] - known) / upper[row_index, row_index])

    return lax.fori_loop(0, columns_total, substitute, jnp.zeros((columns_total,), jnp.float32))


def per_device(right_side, initial, reaction, velocity_x, velocity_y):
    row_count, column_count = right_side.shape
    speeds = jnp.stack([velocity_x, velocity_y])
    padded_speeds = padded_2(speeds, (("gx", 1), (GY, 2)), 2, True)

    def operator_on(field):
        padded_field = padded_2(field, (("gx", 0), (GY, 1)), 2, True)
        return apply_operator(field, padded_field, padded_speeds, reaction, velocity_x, velocity_y)

    start_residual = right_side - operator_on(initial)
    start_square = one_axis_at_a_time(jnp.sum(start_residual * start_residual), GX_GY)
    beta = jnp.sqrt(start_square)
    basis = jnp.zeros((RESTART + 1, row_count, column_count), jnp.float32)
    basis = basis.at[0].set(start_residual / beta)
    hessenberg = jnp.zeros((RESTART + 1, RESTART), jnp.float32)
    positions = jnp.arange(RESTART + 1)

    def arnoldi(column, carried):
        basis, hessenberg = carried
        current = lax.dynamic_index_in_dim(basis, column, 0, keepdims=False)
        applied = operator_on(current)
        local_projection = jnp.einsum("kxy,xy->k", basis, applied, precision=lax.Precision.HIGHEST)
        projection, applied_square = (
            one_axis_at_a_time(local_projection, GX_GY),
            one_axis_at_a_time(jnp.sum(applied * applied), GX_GY),
        )
        applied = applied - jnp.einsum(
            "k,kxy->xy", projection, basis, precision=lax.Precision.HIGHEST
        )
        length = jnp.sqrt(applied_square - jnp.sum(projection * projection))
        entries = jnp.where(positions == column + 1, length, projection)
        hessenberg = lax.dynamic_update_slice(hessenberg, entries[:, None], (0, column))
        basis = lax.dynamic_update_index_in_dim(basis, applied / length, column + 1, 0)
        return (basis, hessenberg)

    basis, hessenberg = lax.fori_loop(0, RESTART, arnoldi, (basis, hessenberg))
    weights = least_squares(hessenberg, beta)
    padded_weights = jnp.concatenate([weights, jnp.zeros((1,), jnp.float32)])
    solution = initial + jnp.einsum(
        "k,kxy->xy", padded_weights, basis, precision=lax.Precision.HIGHEST
    )
    leftover = jnp.where(positions == 0, beta, 0.0) - jnp.dot(
        hessenberg, weights, precision=lax.Precision.HIGHEST
    )
    residual = jnp.einsum("k,kxy->xy", leftover, basis, precision=lax.Precision.HIGHEST)
    return (solution, residual)


def solution(mesh):
    torus = Mesh(mesh.devices.reshape(mesh.shape["gx"], 4, 4, 4), ("gx", "gy_0", "gy_1", "gy_2"))
    placed = (P("gx", GY), P("gx", GY), P("gx", GY), P("gx", GY), P("gx", GY))
    return jax.shard_map(
        per_device,
        mesh=torus,
        in_specs=placed,
        out_specs=(P("gx", GY), P("gx", GY)),
        check_vma=False,
    )
```

profile of v0, /device:TPU:0, one launch (start us, length us, event | category | flops | bytes accessed | tf_op | source)
XLA Modules:
  0.0 1035.0 jit_solution(6680681950074222786)
XLA Ops:
  3.4 8.8 collective-permute-start.6
  44.3 16.7 %psum.143 = f32[]{:T(128)} all-reduce(f32[]{:T(128)} %psum.142), channel_id=1, replica_groups=mesh['gx'=2,'gy_0'=4,'gy_1'=4,'gy_2'=4] {'gy_2'}, use_global_device_ids=true, to_apply=%region_4.0 | all-reduce | flops 1 | bytes 8 | tf_op jit(solution)/shard_map/psum | solution.py:31
  61.8 747.0 %while.56 = (s32[]{:T(128)}, f32[16,64,256]{2,1,0:T(8,128)S(1)}, f32[16,15]{0,1:T(8,128)S(1)}, f32[64,256]{1,0:T(8,128)S(1)}, f32[64,256]{1,0:T(8,128)S(1)}, /*i...) while((s32[]{:T(128)}, f32[16,64,256]{2,1,0:T(8,128)S(1)}, ...), condition=%wide.region_16.0_spmd.clone, body=%wide.region_5.16_spmd.clone.sunk | while | flops 7373337 | bytes 4410527 | solution.py:135
  95.5 9.4 all-reduce.12
  145.6 9.4 all-reduce.12
  178.9 8.3 all-reduce.10
  187.3 8.3 all-reduce.11
  195.6 9.4 all-reduce.12
  229.0 8.3 all-reduce.10
  237.3 8.3 all-reduce.11
  245.7 9.4 all-reduce.12
  279.0 8.3 all-reduce.10
  287.4 8.3 all-reduce.11
  295.7 9.4 all-reduce.12
  329.1 8.3 all-reduce.10
  337.4 8.3 all-reduce.11
  345.8 9.4 all-reduce.12
  379.1 8.3 all-reduce.10
  387.5 8.3 all-reduce.11
  395.8 9.4 all-reduce.12
  429.2 8.3 all-reduce.10
  437.5 8.3 all-reduce.11
  445.9 9.4 all-reduce.12
  495.9 9.4 all-reduce.12
  546.0 9.4 all-reduce.12
  596.0 9.4 all-reduce.12
  646.1 9.4 all-reduce.12
  696.1 9.4 all-reduce.12
  746.2 9.4 all-reduce.12
  796.2 9.4 all-reduce.12
  809.5 162.3 %while.54 = (s32[]{:T(128)}, f32[16,15]{1,0:T(8,128)S(1)}, f32[16]{0:T(128)S(1)}, s32[]{:T(128)}, s32[2]{0:T(128)S(1)}, /*index=5*/s32[1]{0:T(128)}, s32[]{:T(128)}, s32[]{:T(128)}, s32[]{:T(128)}, s32[]{:T(128)}) while((s32[]{:T(128)}, f32[16,15]{1,0:T(8,128)S(1)}, f32[16]{0:T(128)S(1)}, s32[]{:T(128)}, s32[2]{0:T(128)S(1)}, ...), condition=%wide.region_20.21_spmd, body=%wide.region_17.20_spmd.sunk | while | flops 165 | bytes 5167 | solution.py:90
  971.8 59.4 %while.55 = (s32[]{:T(128)}, f32[15]{0:T(128)S(1)}, f32[16]{0:T(128)S(1)}, f32[16,15]{1,0:T(8,128)S(1)}, s32[]{:T(128)}, /*index=5*/s32[]{:T(128)}, s32[]{:T(128)}, s32[]{:T(128)}, s32[]{:T(128)}) while((s32[]{:T(128)}, f32[15]{0:T(128)S(1)}, f32[16]{0:T(128)S(1)}, f32[16,15]{1,0:T(8,128)S(1)}, s32[]{:T(128)}, /*index=5*/s32[]{:T(128)}, ...), condition=%wide.region_23.24_spmd, body=%wide.region_21.23_spmd.sunk | while | flops 43 | bytes 490 | solution.py:97
  (626 shorter events, 617.2 us)
Async XLA Ops:
  1.4 10.8 %collective-permute-start.8 = (f32[2,2,256]{2,1,0:T(2,128)S(1)}, f32[2,2,256]{2,1,0:T(2,128)S(1)}, u32[]{:S(2)}, u32[]{:S(2)}) collective-permute-start(f32[2,2,256]{2,1,0:T(2,128)S(1)} %get-tuple-element.581), channel_id=1, source_target_pairs={{0,64},{64,0},{1,65},{65,1},{2,66},{66,2},{3,67},{67,3},{4,68},{68... | collective-permute-start | bytes 12296 | tf_op jit(solution)/shard_map/ppermute | solution.py:20
  1.4 10.8 %collective-permute-start.9 = (f32[2,2,256]{2,1,0:T(2,128)S(1)}, f32[2,2,256]{2,1,0:T(2,128)S(1)}, u32[]{:S(2)}, u32[]{:S(2)}) collective-permute-start(f32[2,2,256]{2,1,0:T(2,128)S(1)} %get-tuple-element.582), channel_id=1, source_target_pairs={{64,0},{0,64},{65,1},{1,65},{66,2},{2,66},{67,3},{3,67},{68,4},{4,... | collective-permute-start | bytes 12296 | tf_op jit(solution)/shard_map/ppermute | solution.py:22
  3.4 16.6 %collective-permute-start.6 = (f32[68,2]{1,0:T(8,128)S(1)}, f32[68,2]{1,0:T(8,128)S(1)}, u32[]{:S(2)}, u32[]{:S(2)}) collective-permute-start(f32[68,2]{1,0:T(8,128)S(1)} %get-tuple-element.584), channel_id=1, source_target_pairs={{1,0},{2,1},{3,2},{4,3},{5,4},{6,5},{7,6},{8,7},{9,8},{10,9},{11,1... | collective-permute-start | bytes 1640 | tf_op jit(solution)/shard_map/ppermute | solution.py:22
  12.2 9.7 collective-permute-start.7
  12.4 10.3 collective-permute-start.10
  12.4 10.2 collective-permute-start.11
  63.4 9.5 collective-permute-start.3
  109.7 5.5 collective-permute-start.2
  113.5 9.4 collective-permute-start.3
  159.8 5.5 collective-permute-start.2
  163.6 9.4 collective-permute-start.3
  209.8 5.5 collective-permute-start.2
  213.6 9.4 collective-permute-start.3
  259.9 5.5 collective-permute-start.2
  263.7 9.4 collective-permute-start.3
  313.7 9.4 collective-permute-start.3
  360.0 5.5 collective-permute-start.2
  363.8 9.4 collective-permute-start.3
  413.8 9.4 collective-permute-start.3
  460.1 5.5 collective-permute-start.2
  463.9 9.4 collective-permute-start.3
  510.1 5.5 collective-permute-start.2
  513.9 9.4 collective-permute-start.3
  560.2 5.5 collective-permute-start.2
  564.0 9.4 collective-permute-start.3
  610.2 5.5 collective-permute-start.2
  614.0 9.4 collective-permute-start.3
  660.3 5.5 collective-permute-start.2
  664.1 9.4 collective-permute-start.3
  710.3 5.5 collective-permute-start.2
  714.1 9.4 collective-permute-start.3
  764.2 9.4 collective-permute-start.3
  (42 other events, 82.7 us)
where the time goes:
time: 1040 us
  blocking collectives  475 us (46%)
  waiting for transfers between devices  154 us (15%)
  loops' own time  149 us (14%)
  other arithmetic  84.3 us (8%)
  starting transfers between devices  81.7 us (8%)
  matrix products  46.7 us (4%)
  local copies, waits for them, and re-layouts  42.3 us (4%)
    psum x64, blocking collectives, one_axis_at_a_time(): x = lax.psum(x, axis)  475 us
    ppermute x34, waiting for transfers between devices, padded_2(): lax.ppermute(tail, axis, [(i, (i + 1) % count) for i in range(ends)])  119 us
    another operation x1, loops' own time, least_squares(): lax.fori_loop(0, columns_total, rotate, (hessenberg, target))  97.8 us
    ppermute x34, starting transfers between devices, padded_2(): lax.ppermute(head, axis, [((i + 1) % count, i) for i in range(ends)])  71.7 us
    ppermute x34, waiting for transfers between devices, padded_2(): lax.ppermute(head, axis, [((i + 1) % count, i) for i in range(ends)])  35.2 us
    another operation x46, other arithmetic  30.6 us
    another operation x1, loops' own time, least_squares(): lax.fori_loop(0, columns_total, substitute, jnp.zeros((columns_total,), j...  30.2 us
    dot_general x15, matrix products, arnoldi(): jnp.einsum('kxy,xy->k', basis, applied, precision=lax.Precision.HIGHEST)  26.6 us
  transfers between devices with their start and end apart: 68, of which 64 were waited for; matrix products, arithmetic and copies ran while one was open for 0% of the time, Pallas kernels for 0%

commit v1 on v0

--- a/solution.py
+++ b/solution.py
@@ -28,7 +28,8 @@
 
 def one_axis_at_a_time(x, axes):
     for axis in axes:
-        x = lax.psum(x, axis)
+        shards = lax.all_gather(x, axis)
+        x = jnp.sum(shards, axis=0)
     return x
 
 

time: 1040 us -> 1170 us (1.12)
  local copies, waits for them, and re-layouts: 42.3 us -> 188 us
  waiting for transfers between devices: 154 us -> 94.7 us
  other arithmetic: 84.3 us -> 124 us
  loops' own time: 149 us -> 188 us
  blocking collectives: 475 us -> 452 us
  starting transfers between devices: 81.7 us -> 65.1 us
    psum x64 -> x0, blocking collectives: 475 us -> none  [one_axis_at_a_time(): x = lax.psum(x, axis)]
    while x0 -> x60, blocking collectives: none -> 418 us
    while x30 -> x330, local copies, waits for them, and re-layouts: 0.12 us -> 132 us
    reduce_sum x0 -> x124, other arithmetic: none -> 39.8 us  [one_axis_at_a_time(): x = jnp.sum(shards, axis=0)]
    another operation x1, loops' own time: 21 us -> 59.5 us  [per_device(): basis, hessenberg = lax.fori_loop(0, RESTART, arnoldi, (basis, hessenberg))]
    ppermute x34, waiting for transfers between devices: 35.2 us -> 0.09 us  [padded_2(): lax.ppermute(head, axis, [((i + 1) % count, i) for i in range(ends)])]
    unnamed x0 -> x4, blocking collectives: none -> 34.2 us
    ppermute x34, waiting for transfers between devices: 119 us -> 94.6 us  [padded_2(): lax.ppermute(tail, axis, [(i, (i + 1) % count) for i in range(ends)])]
  transfers between devices with their start and end apart: 68 -> 68, of which waited for: 64 -> 17; matrix products, arithmetic and copies ran while one was open for 0% -> 3% of each run, Pallas kernels for 0% -> 0%
where the time goes in v1:
time: 1170 us; the launch traced here: 1160 us
  blocking collectives  452 us (39%)
  local copies, waits for them, and re-layouts  188 us (16%)
  loops' own time  188 us (16%)
  other arithmetic  124 us (11%)
  waiting for transfers between devices  94.7 us (8%)
  starting transfers between devices  65.1 us (6%)
  matrix products  46.7 us (4%)
    while x60, blocking collectives  418 us
    while x330, local copies, waits for them, and re-layouts  132 us
    another operation x1, loops' own time, least_squares(): lax.fori_loop(0, columns_total, rotate, (hessenberg, target))  97.9 us
    ppermute x34, waiting for transfers between devices, padded_2(): lax.ppermute(tail, axis, [(i, (i + 1) % count) for i in range(ends)])  94.6 us
    another operation x1, loops' own time, per_device(): basis, hessenberg = lax.fori_loop(0, RESTART, arnoldi, (basis, hessenberg))  59.5 us
    ppermute x34, starting transfers between devices, padded_2(): lax.ppermute(head, axis, [((i + 1) % count, i) for i in range(ends)])  55.1 us
    reduce_sum x124, other arithmetic, one_axis_at_a_time(): x = jnp.sum(shards, axis=0)  39.8 us
    unnamed x4, blocking collectives  34.2 us
  transfers between devices with their start and end apart: 68, of which 17 were waited for; matrix products, arithmetic and copies ran while one was open for 3% of the time, Pallas kernels for 0%

profile of v1, /device:TPU:0, one launch (start us, length us, event | category | flops | bytes accessed | tf_op | source)
XLA Modules:
  0.0 1159.9 jit_solution(2745572565261197550)
XLA Ops:
  3.9 8.8 collective-permute-start.6
  52.3 16.3 %all-reduce.12 = f32[4]{0:T(128)S(1)} all-reduce(f32[4]{0:T(128)S(1)} %dynamic-update-slice.49), channel_id=1, replica_groups=mesh['gx'=2,'gy_0'=4,'gy_1'=4,'gy_2'=4] {'gy_2'}, use_global_device_ids=true, to_apply=%add.12 | all-reduce | flops 4 | bytes 32
  70.1 863.7 %while.56 = (s32[]{:T(128)}, f32[16,64,256]{2,1,0:T(8,128)S(1)}, f32[16,15]{0,1:T(8,128)S(1)}, f32[64,256]{1,0:T(8,128)S(1)}, f32[64,256]{1,0:T(8,128)S(1)}, /*i...) while((s32[]{:T(128)}, f32[16,64,256]{2,1,0:T(8,128)S(1)}, ...), condition=%wide.region_16.0_spmd.clone, body=%wide.region_5.16_spmd.clone.sunk | while | flops 7373683 | bytes 4416671 | solution.py:136
  111.3 10.0 all-reduce.32
  149.1 7.7 all-reduce.30
  159.1 7.7 all-reduce.31
  169.1 10.0 all-reduce.32
  226.8 10.0 all-reduce.32
  264.6 7.7 all-reduce.30
  274.6 7.7 all-reduce.31
  284.6 10.0 all-reduce.32
  332.4 7.7 all-reduce.31
  342.3 10.0 all-reduce.32
  380.1 7.7 all-reduce.30
  400.1 10.0 all-reduce.32
  437.9 7.7 all-reduce.30
  447.8 7.7 all-reduce.31
  457.8 10.0 all-reduce.32
  515.6 10.0 all-reduce.32
  553.4 7.7 all-reduce.30
  563.3 7.7 all-reduce.31
  573.3 10.0 all-reduce.32
  621.1 7.7 all-reduce.31
  631.1 10.0 all-reduce.32
  668.9 7.7 all-reduce.30
  688.8 10.0 all-reduce.32
  746.6 10.0 all-reduce.32
  804.3 10.0 all-reduce.32
  862.1 10.0 all-reduce.32
  919.8 10.0 all-reduce.32
  934.4 162.3 %while.54 = (s32[]{:T(128)}, f32[16,15]{1,0:T(8,128)S(1)}, f32[16]{0:T(128)S(1)}, s32[]{:T(128)}, s32[2]{0:T(128)S(1)}, /*index=5*/s32[1]{0:T(128)}, s32[]{:T(128)}, s32[]{:T(128)}, s32[]{:T(128)}, s32[]{:T(128)}) while((s32[]{:T(128)}, f32[16,15]{1,0:T(8,128)S(1)}, f32[16]{0:T(128)S(1)}, s32[]{:T(128)}, s32[2]{0:T(128)S(1)}, ...), condition=%wide.region_20.21_spmd, body=%wide.region_17.20_spmd.sunk | while | flops 165 | bytes 5167 | solution.py:91
  1096.7 59.4 %while.55 = (s32[]{:T(128)}, f32[15]{0:T(128)S(1)}, f32[16]{0:T(128)S(1)}, f32[16,15]{1,0:T(8,128)S(1)}, s32[]{:T(128)}, /*index=5*/s32[]{:T(128)}, s32[]{:T(128)}, s32[]{:T(128)}, s32[]{:T(128)}) while((s32[]{:T(128)}, f32[15]{0:T(128)S(1)}, f32[16]{0:T(128)S(1)}, f32[16,15]{1,0:T(8,128)S(1)}, s32[]{:T(128)}, /*index=5*/s32[]{:T(128)}, ...), condition=%wide.region_23.24_spmd, body=%wide.region_21.23_spmd.sunk | while | flops 43 | bytes 490 | solution.py:98
  (1130 shorter events, 703.2 us)
Async XLA Ops:
  1.4 11.3 collective-permute-start.8
  1.4 11.3 collective-permute-start.9
  3.9 16.6 %collective-permute-start.6 = (f32[68,2]{1,0:T(8,128)S(1)}, f32[68,2]{1,0:T(8,128)S(1)}, u32[]{:S(2)}, u32[]{:S(2)}) collective-permute-start(f32[68,2]{1,0:T(8,128)S(1)} %get-tuple-element.584), channel_id=1, source_target_pairs={{1,0},{2,1},{3,2},{4,3},{5,4},{6,5},{7,6},{8,7},{9,8},{10,9},{11,1... | collective-permute-start | bytes 1640 | tf_op jit(solution)/shard_map/ppermute | solution.py:22
  12.7 9.4 collective-permute-start.7
  12.9 10.1 collective-permute-start.10
  12.9 10.0 collective-permute-start.11
  72.7 9.5 collective-permute-start.3
  127.9 5.7 collective-permute-start.2
  130.5 9.4 collective-permute-start.3
  185.7 5.7 collective-permute-start.2
  188.3 9.4 collective-permute-start.3
  243.4 5.7 collective-permute-start.2
  246.0 9.4 collective-permute-start.3
  301.2 5.7 collective-permute-start.2
  303.8 9.4 collective-permute-start.3
  358.9 5.7 collective-permute-start.2
  361.5 9.4 collective-permute-start.3
  416.6 5.7 collective-permute-start.2
  419.3 9.4 collective-permute-start.3
  474.4 5.7 collective-permute-start.2
  477.0 9.4 collective-permute-start.3
  532.1 5.7 collective-permute-start.2
  534.8 9.4 collective-permute-start.3
  592.5 9.4 collective-permute-start.3
  647.6 5.7 collective-permute-start.2
  650.3 9.4 collective-permute-start.3
  708.0 9.4 collective-permute-start.3
  763.1 5.7 collective-permute-start.2
  765.8 9.4 collective-permute-start.3
  823.5 9.4 collective-permute-start.3
  878.6 5.7 collective-permute-start.2
  881.3 9.4 collective-permute-start.3
  (46 other events, 126.1 us)
